TPU v7x, 128 devices: a whole 4x4x4 slice. The times are simulated.
128 devices in a mesh: shard: 128 (over x, z, y, core).
Axes of the slice: x: 4, y: 4, z: 4, core: 2. Of those that a mesh axis runs over, the one named last changes fastest.
Arguments:
- lookup_ids: int32 [262144], P('shard'), may hold values from 0 to 2097151, as said below
- grad_rows: float32 [262144, 128], P('shard'), may hold values from -6 to 6
- emb_table: float32 [2097152, 128], P('shard'), may hold values from -4 to 4
- row_accum: float32 [2097152], P('shard'), may hold values from 0.01 to 1
Outputs:
- new_table: float32 [2097152, 128], P('shard')
- new_accum: float32 [2097152], P('shard')
- looked_up: float32 [262144, 128], P('shard')
Inputs may be any that keep to these rules, and one draw needn't show every extreme that they name: `lookup_ids`: each device's 2048 lookups name exactly 16 rows, repeats counted, in the range of every owner; within an owner's range the row numbers follow a power law, so that a few rows are named very often.
All inputs are finite; a program needn't handle non-finite values.
Results may differ from a plain program's by a relative error of at most 0.00002.
Values sent between devices are 32-bit elements; how exact they have to be, the bound alone decides.
A program may use at most 64 MiB of HBM per device.

v0:
```python
import jax
import jax.numpy as jnp
from jax import lax
from jax.sharding import PartitionSpec as P

LEARNING_RATE = 0.5
EPSILON = 1e-08


def on_device(lookup_ids, grad_rows, emb_table, row_accum):
    peer_count = lax.axis_size("shard")
    look_count = lookup_ids.shape[0]
    row_width = grad_rows.shape[1]
    rows_dev = emb_table.shape[0]
    per_peer = look_count // peer_count
    owners = lookup_ids // rows_dev
    offsets = lookup_ids - owners * rows_dev
    arrange = jnp.argsort(owners, stable=True)
    send_offsets = offsets[arrange].astype(jnp.float32).reshape(peer_count, per_peer)
    send_grads = grad_rows[arrange].reshape(peer_count, per_peer, row_width)
    recv_offsets, recv_grads = (
        lax.all_to_all(send_offsets, "shard", split_axis=0, concat_axis=0, tiled=True),
        lax.all_to_all(send_grads, "shard", split_axis=0, concat_axis=0, tiled=True),
    )
    local_rows = recv_offsets.reshape(-1).astype(jnp.int32)
    flat_grads = recv_grads.reshape(-1, row_width)
    summed = jax.ops.segment_sum(flat_grads, local_rows, num_segments=rows_dev)
    new_accum = row_accum + jnp.mean(summed * summed, axis=1)
    new_table = emb_table - LEARNING_RATE * summed / (jnp.sqrt(new_accum)[:, None] + EPSILON)
    fresh_rows = new_table[local_rows].reshape(peer_count, per_peer, row_width)
    returned = lax.all_to_all(fresh_rows, "shard", split_axis=0, concat_axis=0, tiled=True).reshape(
        look_count, row_width
    )
    looked_up = jnp.zeros_like(grad_rows).at[arrange].set(returned)
    return (new_table, new_accum, looked_up)


def solution(mesh):
    in_specs = (P("shard"), P("shard", None), P("shard", None), P("shard"))
    out_specs = (P("shard", None), P("shard"), P("shard", None))
    return jax.shard_map(
        on_device, mesh=mesh, in_specs=in_specs, out_specs=out_specs, check_vma=False
    )
```

profile of v0, /device:TPU:1, one launch (start us, length us, event | category | flops | bytes accessed | tf_op | source)
XLA Modules:
  0.0 135.3 jit_solution(3246467530488286573)
XLA Ops:
  0.6 0.0 copy-start
  0.6 0.8 add_select_fusion
  1.4 5.0 %sort.17 = (s32[2048]{0:T(1024)}, s32[2048]{0:T(1024)S(1)}) sort(s32[2048]{0:T(1024)S(1)} %get-tuple-element.9, s32[2048]{0:T(1024)S(1)} %iota.4), dimensions={0}, to_apply=%region_0.1 | sort | flops 22528 | bytes 32768 | tf_op jit(solution)/shard_map/jit(argsort)/sort | solution.py:18
  6.5 11.8 %gather_fusion = s32[2048]{0:T(1024)S(1)} fusion(s32[2048]{0:T(1024)S(1)} %get-tuple-element.10, s32[2048]{0:T(1024)S(1)} %get-tuple-element.8), kind=kCustom, calls=%fused_computation | custom fusion | bytes 24576 | tf_op jit(solution)/shard_map/gather | solution.py:19
  18.3 0.7 convert_element_type.32
  19.0 11.5 %all-to-all-start = ((f32[128,1,16]{2,1,0:T(1,128)}), f32[128,1,16]{2,1,0:T(1,128)S(1)}, u32[]{:S(2)}, u32[]{:S(2)}) async-start(f32[128,1,16]{2,1,0:T(1,128)} %bitcast), calls=%async_computation | async-start | bytes 131072 | tf_op jit(solution)/shard_map/all_to_all | solution.py:22
  30.5 0.0 copy-done
  30.5 7.6 %gather_fusion.1 = f32[2048,128]{1,0:T(8,128)} fusion(f32[2048,128]{1,0:T(8,128)S(1)} %copy-done, s32[2048]{0:T(1024)S(1)} %get-tuple-element.8), kind=kCustom, calls=%fused_computation.1 | custom fusion | bytes 2105344 | tf_op jit(solution)/shard_map/gather | solution.py:20
  38.1 1.8 %all-to-all-done = f32[128,1,16]{2,1,0:T(1,128)S(1)} async-done(((f32[128,1,16]{2,1,0:T(1,128)}), f32[128,1,16]{2,1,0:T(1,128)S(1)}, u32[]{:S(2)}, u32[]{:S(2)}) %all-to-all-start) | async-done | bytes 8224 | tf_op jit(solution)/shard_map/all_to_all | solution.py:22
  39.9 8.0 %all-to-all-start.1 = ((f32[128,16,128]{2,1,0:T(8,128)}), f32[128,16,128]{2,1,0:T(8,128)S(1)}, u32[]{:S(2)}, u32[]{:S(2)}) async-start(f32[128,16,128]{2,1,0:T(8,128)} %bitcast.1), calls=%async_computation.1 | async-start | bytes 2097152 | tf_op jit(solution)/shard_map/all_to_all | solution.py:23
  47.9 0.2 convert_reduce_fusion
  48.1 0.1 reshape.92
  48.2 0.1 convert_element_type.34
  48.4 18.6 %all-to-all-done.1 = f32[128,16,128]{2,1,0:T(8,128)S(1)} async-done(((f32[128,16,128]{2,1,0:T(8,128)}), f32[128,16,128]{2,1,0:T(8,128)S(1)}, u32[]{:S(2)}, u32[]{:S(2)}) %all-to-all-start.1) | async-done | bytes 1048608 | tf_op jit(solution)/shard_map/all_to_all | solution.py:23
  66.9 0.0 copy-start.2
  66.9 15.3 %scatter_custom_fusion = f32[16384,128]{1,0:T(8,128)} fusion(s32[2048]{0:T(1024)S(1)} %reshape.92, f32[2048,128]{1,0:T(8,128)S(1)} %bitcast.9, f32[]{:T(128)} %constant.11.clone.1), kind=kCustom, calls=%fused_computation.7 | custom fusion | flops 262144 | bytes 8388612 | tf_op jit(solution)/shard_map/scatter-add | solution.py:27
  82.3 0.0 copy-start.1
  82.3 5.4 %multiply_reduce_fusion = f32[16384]{0:T(1024)S(1)} fusion(f32[16384,128]{1,0:T(8,128)} %scatter_custom_fusion), kind=kLoop, calls=%fused_computation.6 | loop fusion | flops 4177920 | bytes 8454144 | tf_op jit(solution)/shard_map/reduce_sum | solution.py:28
  87.7 0.0 copy-done.2
  87.7 0.6 sqrt_add_fusion
  88.4 0.0 copy-done.1
  88.4 8.0 %divide_subtract_fusion = f32[16384,128]{1,0:T(8,128)} fusion(f32[16384,128]{1,0:T(8,128)} %param.6, f32[16384,128]{1,0:T(8,128)S(1)} %copy-done.1, f32[16384]{0:T(1024)S(1)} %get-tuple-element.5), kind=kLoop, calls=%fused_computation.5 | loop fusion | flops 6291456 | bytes 25231360 | tf_op jit(solution)/shard_map/sub | solution.py:29
  96.3 8.8 %gather_fusion.2 = f32[2048,128]{1,0:T(8,128)S(1)} fusion(f32[16384,128]{1,0:T(8,128)} %divide_subtract_fusion, s32[2048]{0:T(1024)S(1)} %broadcast_clamp_fusion), kind=kCustom, calls=%fused_computation.2 | custom fusion | bytes 2105344 | tf_op jit(solution)/shard_map/gather | solution.py:30
  105.2 23.5 %all_to_all.16 = f32[128,16,128]{2,1,0:T(8,128)S(1)} all-to-all(f32[128,16,128]{2,1,0:T(8,128)S(1)} %bitcast.8), channel_id=1, replica_groups=mesh['shard'=128] {'shard'}, dimensions={0} | all-to-all | bytes 2097152 | tf_op jit(solution)/shard_map/all_to_all | solution.py:31
  128.7 6.6 %scatter_custom_fusion.1 = f32[2048,128]{1,0:T(8,128)} fusion(s32[2048]{0:T(1024)S(1)} %get-tuple-element.7, f32[2048,128]{1,0:T(8,128)S(1)} %bitcast.10, f32[]{:T(128)} %constant.11.clone.1), kind=kCustom, calls=%fused_computation.9 | custom fusion | bytes 1048580 | tf_op jit(solution)/shard_map/scatter | solution.py:34
  (6 shorter events, 0.1 us)
Async XLA Ops:
  0.6 29.9 %copy-start = (f32[2048,128]{1,0:T(8,128)S(1)}, f32[2048,128]{1,0:T(8,128)}, u32[]{:S(2)}) copy-start(f32[2048,128]{1,0:T(8,128)} %param.5) | copy-start | bytes 3145732
  19.0 20.9 %all-to-all-start = ((f32[128,1,16]{2,1,0:T(1,128)}), f32[128,1,16]{2,1,0:T(1,128)S(1)}, u32[]{:S(2)}, u32[]{:S(2)}) async-start(f32[128,1,16]{2,1,0:T(1,128)} %bitcast), calls=%async_computation | async-start | bytes 131072 | tf_op jit(solution)/shard_map/all_to_all | solution.py:22
  39.9 27.0 %all-to-all-start.1 = ((f32[128,16,128]{2,1,0:T(8,128)}), f32[128,16,128]{2,1,0:T(8,128)S(1)}, u32[]{:S(2)}, u32[]{:S(2)}) async-start(f32[128,16,128]{2,1,0:T(8,128)} %bitcast.1), calls=%async_computation.1 | async-start | bytes 2097152 | tf_op jit(solution)/shard_map/all_to_all | solution.py:23
  66.9 20.8 %copy-start.2 = (f32[16384]{0:T(1024)S(1)}, f32[16384]{0:T(1024)}, u32[]{:S(2)}) copy-start(f32[16384]{0:T(1024)} %param.7) | copy-start | bytes 196612
  82.3 6.1 %copy-start.1 = (f32[16384,128]{1,0:T(8,128)S(1)}, f32[16384,128]{1,0:T(8,128)}, u32[]{:S(2)}) copy-start(f32[16384,128]{1,0:T(8,128)} %scatter_custom_fusion) | copy-start | bytes 25165828
where the time goes:
time: 136 us; the launch traced here: 135 us
  local copies, waits for them, and re-layouts  35.7 us (26%)
  other arithmetic  35.5 us (26%)
  blocking collectives  23.5 us (17%)
  waiting for transfers between devices  20.4 us (15%)
  starting transfers between devices  19.4 us (14%)
    all_to_all x1, blocking collectives, on_device(): lax.all_to_all(fresh_rows, 'shard', split_axis=0, concat_axis=0, tiled=True)  23.5 us
    all_to_all x1, waiting for transfers between devices, on_device(): lax.all_to_all(send_grads, 'shard', split_axis=0, concat_axis=0, tiled=True)  18.6 us
    scatter-add x1, other arithmetic, on_device(): summed = jax.ops.segment_sum(flat_grads, local_rows, num_segments=rows_dev)  15.3 us
    gather x1, local copies, waits for them, and re-layouts, on_device(): offsets[arrange].astype(jnp.float32).reshape(peer_count, per_peer)  11.8 us
    all_to_all x1, starting transfers between devices, on_device(): lax.all_to_all(send_offsets, 'shard', split_axis=0, concat_axis=0, tiled=...  11.5 us
    gather x1, local copies, waits for them, and re-layouts, on_device(): fresh_rows = new_table[local_rows].reshape(peer_count, per_peer, row_width)  8.84 us
    sub x1, other arithmetic, on_device(): emb_table - LEARNING_RATE * summed / (jnp.sqrt(new_accum)[:, None] + EPSI...  7.98 us
    all_to_all x1, starting transfers between devices, on_device(): lax.all_to_all(send_grads, 'shard', split_axis=0, concat_axis=0, tiled=True)  7.96 us
  transfers between devices with their start and end apart: 2, of which 2 were waited for; matrix products, arithmetic and copies ran while one was open for 6% of the time, Pallas kernels for 0%

commit v1 on v0

v1 whole, which is shorter than its diff:
```python
import functools

import jax
import jax.numpy as jnp
from jax import lax
from jax.experimental import pallas as pl
from jax.experimental.pallas import tpu as pltpu
from jax.sharding import PartitionSpec as P

LEARNING_RATE = 0.5
EPSILON = 1e-08

MESH = pl.DeviceIdType.MESH
N = 128
W = 128
PER = 16
LOOK = N * PER
ROWS = 16384
ROW_BITS = 14
BLK = 128
NB = LOOK // BLK
SB = 256
NSB = LOOK // SB
PEERS_SB = SB // PER
F32, BF16, I32 = jnp.float32, jnp.bfloat16, jnp.int32


def iota(shape, dim):
    return lax.broadcasted_iota(I32, shape, dim)


def split2(x):
    hi = x.astype(BF16)
    return hi, (x - hi.astype(F32)).astype(BF16)


def onehot(mask):
    return jnp.where(mask, 1.0, 0.0).astype(BF16)


def mm(a, b):
    return jnp.dot(a, b, preferred_element_type=F32)


def mm_nt(a, b):
    return lax.dot_general(a, b, (((1,), (1,)), ((), ())), preferred_element_type=F32)


SLOT_OFFSETS = (1, 42, 84, 48, 8, 2, 4)


def offset_of(q):
    out = 0
    for i in range(4):
        if (q >> i) & 1:
            out ^= SLOT_OFFSETS[i]
    return out


def block_offset(t):
    return (t & 1) * 8 + ((t >> 1) & 1) * 2 + ((t >> 2) & 1) * 4


def slot_of(e):
    bit = lambda i: (e >> i) & 1
    q1 = bit(5) ^ bit(4) ^ bit(6)
    q = bit(0) + (q1 << 1) + (bit(6) << 2) + ((bit(4) ^ bit(6)) << 3)
    t = (bit(3) ^ q1) + ((bit(1) ^ q1) << 1) + ((bit(2) ^ bit(6)) << 2)
    return q + (t << 4)


def remote(src, dst, ssem, rsem, device):
    return pltpu.make_async_remote_copy(
        src_ref=src, dst_ref=dst, send_sem=ssem, recv_sem=rsem, device_id=(device,), device_id_type=MESH
    )


def exchange_kernel(
    ids_hbm, grads_hbm, accum_hbm, table_hbm,
    ret_ref, upd_ref, rows_ref, pos_ref, new_accum_ref, table,
    ids_ref, grads_ref, accum_ref, sendbuf, recvbuf, id_send, id_recv, split, eq, emb, rcol, acc_col, cnt_col,
    msq_col, rows_smem,
    id_ssem, id_rsem, g_ssem, g_rsem, r_ssem, r_rsem, smem_sem, in_sem,
):
    me = lax.axis_index("shard")
    barrier = pltpu.get_barrier_semaphore()

    def greet(k, c):
        pl.semaphore_signal(barrier, inc=1, device_id=(me ^ k,), device_id_type=MESH)
        return c

    lax.fori_loop(1, N, greet, 0)

    copies = [
        pltpu.make_async_copy(frm, to, in_sem.at[i])
        for i, (frm, to) in enumerate(
            ((ids_hbm, ids_ref), (grads_hbm, grads_ref), (accum_hbm, accum_ref), (table_hbm, table))
        )
    ]
    for copy in copies:
        copy.start()
    copies[0].wait()

    sub = iota((N, BLK), 0)
    lane = iota((N, BLK), 1)
    upper = onehot(sub <= lane)
    carry = jnp.zeros((N, 1), F32)
    w_hi = jnp.zeros((N, BLK), F32)
    w_lo = jnp.zeros((N, BLK), F32)
    for b in range(NB):
        ids = ids_ref[b : b + 1, :]
        slot = slot_of(lax.shift_right_logical(ids, ROW_BITS) ^ me)
        row = ids & (ROWS - 1)
        own = jnp.where(sub == slot, 1.0, 0.0)
        own_bf = own.astype(BF16)
        count = mm(own_bf, upper) + carry
        carry = carry + jnp.sum(own, axis=1, keepdims=True)
        rank = jnp.sum(own * count, axis=0, keepdims=True).astype(I32) - 1
        pos_ref[b : b + 1, :] = slot * PER + rank
        here = (sub & (PER - 1)) == rank
        q_hi = jnp.where(here, (row >> 7).astype(F32), 0.0).astype(BF16)
        q_lo = jnp.where(here, (row & 127).astype(F32), 0.0).astype(BF16)
        w_hi = w_hi + mm_nt(own_bf, q_hi)
        w_lo = w_lo + mm_nt(own_bf, q_lo)
    w = (w_hi.astype(I32) << 7) + w_lo.astype(I32)
    for d in range(N):
        id_send[d, 0:1, :] = w[d : d + 1, :]

    copies[1].wait()

    def split_grads(b, c):
        at = pl.ds(pl.multiple_of(b * SB, SB), SB)
        hi, lo = split2(grads_ref[at, :])
        split[at, 0:W] = hi
        split[at, W : 2 * W] = lo
        return c

    lax.fori_loop(0, NSB, split_grads, 0)

    def arrange(t, c):
        base = pl.multiple_of(t * SB, SB)
        want = iota((SB, BLK), 0) + base
        total = jnp.zeros((SB, 2 * W), F32)
        for b in range(NB):
            pick = onehot(want == pos_ref[b : b + 1, :])
            total = total + mm(pick, split[b * BLK : (b + 1) * BLK, :])
        sendbuf[pl.ds(base, SB), :] = total[:, 0:W] + total[:, W : 2 * W]
        return c

    lax.fori_loop(0, NSB, arrange, 0)

    def send_block(t, frm, to, ssem, rsem, first):
        far = me ^ block_offset(t)
        for q in range(first, PEERS_SB):
            slot = t * PEERS_SB + q
            remote(frm(slot), to(slot), ssem, rsem, far ^ offset_of(q)).start()

    def slot_rows(ref):
        return lambda slot: ref.at[pl.ds(pl.multiple_of(slot * PER, PER), PER)]

    def send_all(frm, to, ssem, rsem):
        send_block(0, frm, to, ssem, rsem, 1)

        def some(t, c):
            send_block(t, frm, to, ssem, rsem, 0)
            return c

        lax.fori_loop(1, NSB, some, 0)

    id_row = lambda ref: lambda slot: ref.at[slot, pl.ds(0, 1)]

    pl.semaphore_wait(barrier, N - 1)
    send_all(id_row(id_send), id_row(id_recv), id_ssem, id_rsem)
    send_all(slot_rows(sendbuf), slot_rows(recvbuf), g_ssem, g_rsem)
    id_recv[0, 0:1, :] = id_send[0, 0:1, :]
    recvbuf[0:PER, :] = sendbuf[0:PER, :]

    ids_all = remote(
        id_send.at[pl.ds(0, N - 1), pl.ds(0, 1)], id_recv.at[pl.ds(0, N - 1), pl.ds(0, 1)], id_ssem, id_rsem, me
    )
    ids_all.wait_send()
    ids_all.wait_recv()
    keep = (iota((8, BLK), 0) & 7) == (iota((8, BLK), 1) >> 4)
    for b in range(NB):
        got = jnp.concatenate([id_recv[8 * b + i, 0:1, :] for i in range(8)], axis=0)
        rows_ref[b : b + 1, :] = jnp.sum(jnp.where(keep, got, 0), axis=0, keepdims=True)
    to_smem = pltpu.make_async_copy(rows_ref, rows_smem, smem_sem)
    to_smem.start()
    for b in range(NB):
        row = rows_ref[b : b + 1, :].astype(F32)
        rcol[b * BLK : (b + 1) * BLK, :] = jnp.transpose(jnp.broadcast_to(row, (BLK, BLK)))

    copies[2].wait()
    acc_hi, acc_rest = split2(accum_ref[...])
    acc_lo = (accum_ref[...] - acc_hi.astype(F32) - acc_rest.astype(F32)).astype(BF16)
    acc3 = jnp.concatenate([acc_hi, acc_rest, acc_lo], axis=1)

    def build(b, c):
        at = pl.ds(pl.multiple_of(b * BLK, BLK), BLK)
        col = rcol[at, :]
        seen = jnp.zeros((BLK, BLK), F32)
        for o in range(NB):
            same = jnp.where(col == rows_ref[o : o + 1, :].astype(F32), 1.0, 0.0)
            seen = seen + same
            eq[at, o * BLK : (o + 1) * BLK] = same.astype(BF16)
        cnt_col[at, :] = jnp.broadcast_to(jnp.sum(seen, axis=1, keepdims=True), (BLK, BLK))
        num = col.astype(I32)
        lanes = iota((BLK, BLK), 1)
        picked = mm(onehot((num >> 7) == lanes), acc3)
        picked = picked[:, 0:W] + picked[:, W : 2 * W] + picked[:, 2 * W :]
        acc = jnp.sum(jnp.where((num & 127) == lanes, picked, 0.0), axis=1, keepdims=True)
        acc_col[at, :] = jnp.broadcast_to(acc, (BLK, BLK))
        return c

    lax.fori_loop(0, NB, build, 0)

    copies[3].wait()
    to_smem.wait()

    def gather(b, c):
        base = pl.multiple_of(b * BLK, BLK)
        for i in range(BLK):
            r = rows_smem[b, i] & (ROWS - 1)
            emb[pl.ds(base + i, 1), :] = table[pl.ds(r, 1), :]
        return c

    lax.fori_loop(0, NB, gather, 0)

    many = pl.ds(0, (N - 1) * PER)
    all_grads = remote(sendbuf.at[many], recvbuf.at[many], g_ssem, g_rsem, me)
    all_grads.wait_send()
    all_grads.wait_recv()

    def split_recv(b, c):
        at = pl.ds(pl.multiple_of(b * SB, SB), SB)
        hi, lo = split2(recvbuf[at, :])
        split[at, 0:W] = hi
        split[at, W : 2 * W] = lo
        return c

    lax.fori_loop(0, NSB, split_recv, 0)

    def update(t):
        at = pl.ds(pl.multiple_of(t * SB, SB), SB)
        both = mm(eq[at, :], split[...])
        summed = both[:, 0:W] + both[:, W : 2 * W]
        msq = jnp.broadcast_to(jnp.sum(summed * summed, axis=1, keepdims=True), (SB, W)) * (1.0 / W)
        msq_col[at, :] = msq
        upd_ref[at, :] = emb[at, :] - LEARNING_RATE * summed / (jnp.sqrt(acc_col[at, :] + msq) + EPSILON)

    def update_send(t, c):
        update(t)
        send_block(t, slot_rows(upd_ref), slot_rows(ret_ref), r_ssem, r_rsem, 0)
        return c

    update(0)
    send_block(0, slot_rows(upd_ref), slot_rows(ret_ref), r_ssem, r_rsem, 1)
    lax.fori_loop(1, NSB, update_send, 0)
    ret_ref[0:PER, :] = upd_ref[0:PER, :]

    delta = jnp.zeros((N, BLK), F32)
    for b in range(NB):
        at = slice(b * BLK, (b + 1) * BLK)
        lo_row = rcol[at, :].astype(I32) & 127
        term = jnp.where(lo_row == lane, msq_col[at, :] / cnt_col[at, :], 0.0)
        t_hi, t_mid = split2(term)
        t_lo = (term - t_hi.astype(F32) - t_mid.astype(F32)).astype(BF16)
        pick = onehot((rows_ref[b : b + 1, :] >> 7) == sub)
        delta = delta + mm(pick, t_hi) + mm(pick, t_mid) + mm(pick, t_lo)
    new_accum_ref[...] = accum_ref[...] + delta

    back = remote(upd_ref.at[many], ret_ref.at[many], r_ssem, r_rsem, me)
    back.wait_send()
    back.wait_recv()


def place_kernel(
    table_ref, upd_ref, ret_ref, rows_ref, pos_ref, accum_ref,
    new_table_ref, looked_ref, new_accum_ref, table,
    looked, sems,
):
    accum_out = pltpu.make_async_copy(accum_ref, new_accum_ref, sems.at[0])
    accum_out.start()

    def scatter(b, c):
        base = pl.multiple_of(b * BLK, BLK)
        for i in range(BLK):
            table[pl.ds(rows_ref[b, i], 1), :] = upd_ref[pl.ds(base + i, 1), :]
        return c

    lax.fori_loop(0, NB, scatter, 0)
    table_out = pltpu.make_async_copy(table, new_table_ref, sems.at[1])
    table_out.start()

    def unpermute(b, c):
        base = pl.multiple_of(b * BLK, BLK)
        for i in range(BLK):
            looked[pl.ds(base + i, 1), :] = ret_ref[pl.ds(pos_ref[b, i], 1), :]
        return c

    lax.fori_loop(0, NB, unpermute, 0)
    looked_out = pltpu.make_async_copy(looked, looked_ref, sems.at[2])
    looked_out.start()
    accum_out.wait()
    table_out.wait()
    looked_out.wait()


VM = pl.BlockSpec(memory_space=pltpu.VMEM)
SM = pl.BlockSpec(memory_space=pltpu.SMEM)
HBM = pl.BlockSpec(memory_space=pltpu.HBM)


def on_device(lookup_ids, grad_rows, emb_table, row_accum):
    dma = pltpu.SemaphoreType.DMA
    f32 = lambda *s: jax.ShapeDtypeStruct(s, F32)
    i32 = lambda *s: jax.ShapeDtypeStruct(s, I32)
    vmem = lambda *s: pltpu.VMEM(s, F32)
    in_hbm = lambda a: pltpu.with_memory_space_constraint(a, pltpu.HBM)
    ret, upd, rows, pos, stepped, held = pl.pallas_call(
        exchange_kernel,
        out_shape=(f32(LOOK, W), f32(LOOK, W), i32(NB, BLK), i32(NB, BLK), f32(N, BLK), vmem(ROWS, W)),
        in_specs=[HBM, HBM, HBM, HBM],
        out_specs=(VM, VM, VM, VM, VM, VM),
        scratch_shapes=[
            pltpu.VMEM((NB, BLK), I32),
            pltpu.VMEM((LOOK, W), F32),
            pltpu.VMEM((N, BLK), F32),
            pltpu.VMEM((LOOK, W), F32),
            pltpu.VMEM((LOOK, W), F32),
            pltpu.VMEM((N, 8, W), I32),
            pltpu.VMEM((N, 8, W), I32),
            pltpu.VMEM((LOOK, 2 * W), BF16),
            pltpu.VMEM((LOOK, LOOK), BF16),
            pltpu.VMEM((LOOK, W), F32),
            pltpu.VMEM((LOOK, W), F32),
            pltpu.VMEM((LOOK, W), F32),
            pltpu.VMEM((LOOK, W), F32),
            pltpu.VMEM((LOOK, W), F32),
            pltpu.SMEM((NB, BLK), I32),
            dma, dma, dma, dma, dma, dma, dma,
            pltpu.SemaphoreType.DMA((4,)),
        ],
        compiler_params=pltpu.CompilerParams(
            collective_id=0, has_side_effects=True, vmem_limit_bytes=28 * 1024 * 1024
        ),
    )(*map(in_hbm, (lookup_ids.reshape(NB, BLK), grad_rows, row_accum.reshape(N, BLK), emb_table)))
    new_table, looked_up, new_accum, _ = pl.pallas_call(
        place_kernel,
        out_shape=(f32(ROWS, W), f32(LOOK, W), f32(N, BLK), vmem(ROWS, W)),
        in_specs=[VM, VM, VM, SM, SM, VM],
        out_specs=(HBM, HBM, HBM, VM),
        input_output_aliases={0: 3},
        scratch_shapes=[pltpu.VMEM((LOOK, W), F32), pltpu.SemaphoreType.DMA((3,))],
        compiler_params=pltpu.CompilerParams(vmem_limit_bytes=4 * 1024 * 1024),
    )(held, upd, ret, rows, pos, stepped)
    return (new_table, new_accum.reshape(ROWS), looked_up)


def solution(mesh):
    in_specs = (P("shard"), P("shard", None), P("shard", None), P("shard"))
    out_specs = (P("shard", None), P("shard"), P("shard", None))
    return jax.shard_map(
        on_device, mesh=mesh, in_specs=in_specs, out_specs=out_specs, check_vma=False
    )
```

time: 136 us -> 56 us (0.41)
  Pallas kernels: 0 us -> 55.2 us
  local copies, waits for them, and re-layouts: 35.7 us -> 0 us
  other arithmetic: 35.5 us -> 0 us
  blocking collectives: 23.5 us -> 0 us
  waiting for transfers between devices: 20.4 us -> 0 us
  starting transfers between devices: 19.4 us -> 0 us
    pallas_call x0 -> x2, Pallas kernels: none -> 55.2 us  [the longest x1 49 us: on_device(): pl.pallas_call(exchange_kernel, out_shape=(f32(LOOK, W), f32(LOOK, W), i3...]
    gather x3 -> x0, local copies, waits for them, and re-layouts: 28.3 us -> none  [the longest x1 11.8 us: on_device(): offsets[arrange].astype(jnp.float32).reshape(peer_count, per_peer)]
    all_to_all x1 -> x0, blocking collectives: 23.5 us -> none  [on_device(): lax.all_to_all(fresh_rows, 'shard', split_axis=0, concat_axis=0, tiled=True)]
    all_to_all x2 -> x0, waiting for transfers between devices: 20.4 us -> none  [the longest x1 18.6 us: on_device(): lax.all_to_all(send_grads, 'shard', split_axis=0, concat_axis=0, tiled=True)]
    all_to_all x2 -> x0, starting transfers between devices: 19.4 us -> none  [the longest x1 11.5 us: on_device(): lax.all_to_all(send_offsets, 'shard', split_axis=0, concat_axis=0, tiled=...]
    scatter-add x1 -> x0, other arithmetic: 15.3 us -> none  [on_device(): summed = jax.ops.segment_sum(flat_grads, local_rows, num_segments=rows_dev)]
    sub x1 -> x0, other arithmetic: 7.98 us -> none  [on_device(): emb_table - LEARNING_RATE * summed / (jnp.sqrt(new_accum)[:, None] + EPSI...]
    scatter x1 -> x0, local copies, waits for them, and re-layouts: 6.57 us -> none  [on_device(): looked_up = jnp.zeros_like(grad_rows).at[arrange].set(returned)]
  transfers between devices with their start and end apart: 2 -> 0, of which waited for: 2 -> 0; matrix products, arithmetic and copies ran while one was open for 6% -> 0% of each run, Pallas kernels for 0% -> 0%
where the time goes in v1:
time: 56 us; the launch traced here: 55.9 us
  Pallas kernels  55.2 us (99%)
  between operations  0.64 us (1%)
    pallas_call x1, Pallas kernels, on_device(): pl.pallas_call(exchange_kernel, out_shape=(f32(LOOK, W), f32(LOOK, W), i3...  49 us
    pallas_call x1, Pallas kernels, on_device(): pl.pallas_call(place_kernel, out_shape=(f32(ROWS, W), f32(LOOK, W), f32(N...  6.24 us

profile of v1, /device:TPU:1, one launch (start us, length us, event | category | flops | bytes accessed | tf_op | source)
XLA Modules:
  0.0 55.9 jit_solution(9259551057617332991)
XLA Ops:
  0.6 49.0 %shard_map.67 = (f32[2048,128]{1,0:T(8,128)S(1)}, f32[2048,128]{1,0:T(8,128)S(1)}, s32[16,128]{1,0:T(8,128)S(1)}, s32[16,128]{1,0:T(8,128)S(1)}, f32[128,128]{1,0:T(8,128)S(1)}, /*index=5*/f32[16384,128]{1,0:T(8,128)S(1)}) custom-call(s32[16,128]{1,0:T(8,128)} %bitcast.4, f32[2048,128]{1,0:T(8,128)} %grads_hbm.1, f32[128,128]{1,0:T(8,128)} %bitcast.3, ...), custom_call_target="tpu_custom_call" | custom-call | tf_op jit(solution)/shard_map/pallas_call | solution.py:320
  49.6 6.2 %shard_map.68 = (f32[16384,128]{1,0:T(8,128)}, f32[2048,128]{1,0:T(8,128)}, f32[128,128]{1,0:T(8,128)}, f32[16384,128]{1,0:T(8,128)S(1)}) custom-call(f32[16384,128]{1,0:T(8,128)S(1)} %get-tuple-element.12.table_ref, f32[2048,128]{1,0:T(8,128)S(1)} %get-tuple-element.13.upd_ref, ...), custom_call_target="tpu_custom_call", output_to_operand_aliasing={{3}: (0, {})} | custom-call | tf_op jit(solution)/shard_map/pallas_call | solution.py:348

commit v2 on v1

--- a/solution.py
+++ b/solution.py
@@ -137,7 +137,7 @@
 
     lax.fori_loop(0, NSB, split_grads, 0)
 
-    def arrange(t, c):
+    def arrange(t):
         base = pl.multiple_of(t * SB, SB)
         want = iota((SB, BLK), 0) + base
         total = jnp.zeros((SB, 2 * W), F32)
@@ -145,9 +145,6 @@
             pick = onehot(want == pos_ref[b : b + 1, :])
             total = total + mm(pick, split[b * BLK : (b + 1) * BLK, :])
         sendbuf[pl.ds(base, SB), :] = total[:, 0:W] + total[:, W : 2 * W]
-        return c
-
-    lax.fori_loop(0, NSB, arrange, 0)
 
     def send_block(t, frm, to, ssem, rsem, first):
         far = me ^ block_offset(t)
@@ -169,9 +166,17 @@
 
     id_row = lambda ref: lambda slot: ref.at[slot, pl.ds(0, 1)]
 
+    arrange(0)
     pl.semaphore_wait(barrier, N - 1)
+    send_block(0, slot_rows(sendbuf), slot_rows(recvbuf), g_ssem, g_rsem, 1)
     send_all(id_row(id_send), id_row(id_recv), id_ssem, id_rsem)
-    send_all(slot_rows(sendbuf), slot_rows(recvbuf), g_ssem, g_rsem)
+
+    def arrange_send(t, c):
+        arrange(t)
+        send_block(t, slot_rows(sendbuf), slot_rows(recvbuf), g_ssem, g_rsem, 0)
+        return c
+
+    lax.fori_loop(1, NSB, arrange_send, 0)
     id_recv[0, 0:1, :] = id_send[0, 0:1, :]
     recvbuf[0:PER, :] = sendbuf[0:PER, :]
 

time: 56 us -> 51 us (0.911)
  Pallas kernels: 55.2 us -> 50.3 us
    pallas_call x1, Pallas kernels: 49 us -> 44 us  [on_device(): pl.pallas_call(exchange_kernel, out_shape=(f32(LOOK, W), f32(LOOK, W), i3...]
where the time goes in v2:
time: 51 us; the launch traced here: 50.9 us
  Pallas kernels  50.3 us (99%)
  between operations  0.64 us (1%)
    pallas_call x1, Pallas kernels, on_device(): pl.pallas_call(exchange_kernel, out_shape=(f32(LOOK, W), f32(LOOK, W), i3...  44 us
    pallas_call x1, Pallas kernels, on_device(): pl.pallas_call(place_kernel, out_shape=(f32(ROWS, W), f32(LOOK, W), f32(N...  6.24 us

profile of v2, /device:TPU:1, one launch (start us, length us, event | category | flops | bytes accessed | tf_op | source)
XLA Modules:
  0.0 50.9 jit_solution(4474980749811401419)
XLA Ops:
  0.6 44.0 %shard_map.67 = (f32[2048,128]{1,0:T(8,128)S(1)}, f32[2048,128]{1,0:T(8,128)S(1)}, s32[16,128]{1,0:T(8,128)S(1)}, s32[16,128]{1,0:T(8,128)S(1)}, f32[128,128]{1,0:T(8,128)S(1)}, /*index=5*/f32[16384,128]{1,0:T(8,128)S(1)}) custom-call(s32[16,128]{1,0:T(8,128)} %bitcast.4, f32[2048,128]{1,0:T(8,128)} %grads_hbm.1, f32[128,128]{1,0:T(8,128)} %bitcast.3, ...), custom_call_target="tpu_custom_call" | custom-call | tf_op jit(solution)/shard_map/pallas_call | solution.py:325
  44.7 6.2 %shard_map.68 = (f32[16384,128]{1,0:T(8,128)}, f32[2048,128]{1,0:T(8,128)}, f32[128,128]{1,0:T(8,128)}, f32[16384,128]{1,0:T(8,128)S(1)}) custom-call(f32[16384,128]{1,0:T(8,128)S(1)} %get-tuple-element.12.table_ref, f32[2048,128]{1,0:T(8,128)S(1)} %get-tuple-element.13.upd_ref, ...), custom_call_target="tpu_custom_call", output_to_operand_aliasing={{3}: (0, {})} | custom-call | tf_op jit(solution)/shard_map/pallas_call | solution.py:353

commit v3 on v2

--- a/solution.py
+++ b/solution.py
@@ -61,6 +61,13 @@
     return (t & 1) * 8 + ((t >> 1) & 1) * 2 + ((t >> 2) & 1) * 4
 
 
+def hops(k):
+    return sum((0, 1, 2, 1)[(k >> i) & 3] for i in (1, 3, 5))
+
+
+FAR_FIRST = sorted(range(1, N), key=lambda k: -hops(k))
+
+
 def slot_of(e):
     bit = lambda i: (e >> i) & 1
     q1 = bit(5) ^ bit(4) ^ bit(6)
@@ -77,19 +84,16 @@
 
 def exchange_kernel(
     ids_hbm, grads_hbm, accum_hbm, table_hbm,
-    ret_ref, upd_ref, rows_ref, pos_ref, new_accum_ref, table,
-    ids_ref, grads_ref, accum_ref, sendbuf, recvbuf, id_send, id_recv, split, eq, emb, rcol, acc_col, cnt_col,
-    msq_col, rows_smem,
+    ret_ref, upd_ref, rows_smem, pos_smem, new_accum_ref, table,
+    rows_ref, pos_ref, first, ids_ref, grads_ref, accum_ref, sendbuf, recvbuf, id_send, id_recv, split, eq, emb, rcol, acc_col, cnt_col,
+    msq_col,
     id_ssem, id_rsem, g_ssem, g_rsem, r_ssem, r_rsem, smem_sem, in_sem,
 ):
     me = lax.axis_index("shard")
     barrier = pltpu.get_barrier_semaphore()
 
-    def greet(k, c):
+    for k in FAR_FIRST:
         pl.semaphore_signal(barrier, inc=1, device_id=(me ^ k,), device_id_type=MESH)
-        return c
-
-    lax.fori_loop(1, N, greet, 0)
 
     copies = [
         pltpu.make_async_copy(frm, to, in_sem.at[i])
@@ -97,7 +101,7 @@
             ((ids_hbm, ids_ref), (grads_hbm, grads_ref), (accum_hbm, accum_ref), (table_hbm, table))
         )
     ]
-    for copy in copies:
+    for copy in copies[:3]:
         copy.start()
     copies[0].wait()
 
@@ -105,28 +109,36 @@
     lane = iota((N, BLK), 1)
     upper = onehot(sub <= lane)
     carry = jnp.zeros((N, 1), F32)
-    w_hi = jnp.zeros((N, BLK), F32)
-    w_lo = jnp.zeros((N, BLK), F32)
+
+    def slots_at(b):
+        return slot_of(lax.shift_right_logical(ids_ref[b : b + 1, :], ROW_BITS) ^ me)
+
     for b in range(NB):
-        ids = ids_ref[b : b + 1, :]
-        slot = slot_of(lax.shift_right_logical(ids, ROW_BITS) ^ me)
-        row = ids & (ROWS - 1)
+        slot = slots_at(b)
         own = jnp.where(sub == slot, 1.0, 0.0)
-        own_bf = own.astype(BF16)
-        count = mm(own_bf, upper) + carry
+        count = mm(own.astype(BF16), upper) + carry
         carry = carry + jnp.sum(own, axis=1, keepdims=True)
         rank = jnp.sum(own * count, axis=0, keepdims=True).astype(I32) - 1
         pos_ref[b : b + 1, :] = slot * PER + rank
-        here = (sub & (PER - 1)) == rank
-        q_hi = jnp.where(here, (row >> 7).astype(F32), 0.0).astype(BF16)
-        q_lo = jnp.where(here, (row & 127).astype(F32), 0.0).astype(BF16)
-        w_hi = w_hi + mm_nt(own_bf, q_hi)
-        w_lo = w_lo + mm_nt(own_bf, q_lo)
-    w = (w_hi.astype(I32) << 7) + w_lo.astype(I32)
-    for d in range(N):
-        id_send[d, 0:1, :] = w[d : d + 1, :]
+
+    def pack_ids():
+        w_hi = jnp.zeros((N, BLK), F32)
+        w_lo = jnp.zeros((N, BLK), F32)
+        for b in range(NB):
+            pos = pos_ref[b : b + 1, :]
+            row = ids_ref[b : b + 1, :] & (ROWS - 1)
+            own = onehot(sub == lax.shift_right_logical(pos, 4))
+            here = (sub & (PER - 1)) == (pos & (PER - 1))
+            q_hi = jnp.where(here, (row >> 7).astype(F32), 0.0).astype(BF16)
+            q_lo = jnp.where(here, (row & 127).astype(F32), 0.0).astype(BF16)
+            w_hi = w_hi + mm_nt(own, q_hi)
+            w_lo = w_lo + mm_nt(own, q_lo)
+        w = (w_hi.astype(I32) << 7) + w_lo.astype(I32)
+        for d in range(N):
+            id_send[d, 0:1, :] = w[d : d + 1, :]
 
     copies[1].wait()
+    copies[3].start()
 
     def split_grads(b, c):
         at = pl.ds(pl.multiple_of(b * SB, SB), SB)
@@ -168,15 +180,21 @@
 
     arrange(0)
     pl.semaphore_wait(barrier, N - 1)
-    send_block(0, slot_rows(sendbuf), slot_rows(recvbuf), g_ssem, g_rsem, 1)
+    send_block(0, slot_rows(sendbuf), slot_rows(recvbuf), g_ssem, g_rsem.at[0], 1)
+    pack_ids()
     send_all(id_row(id_send), id_row(id_recv), id_ssem, id_rsem)
 
     def arrange_send(t, c):
         arrange(t)
-        send_block(t, slot_rows(sendbuf), slot_rows(recvbuf), g_ssem, g_rsem, 0)
+        send_block(t, slot_rows(sendbuf), slot_rows(recvbuf), g_ssem, g_rsem.at[t], 0)
         return c
 
     lax.fori_loop(1, NSB, arrange_send, 0)
+    to_smem = [
+        pltpu.make_async_copy(frm, to, smem_sem.at[i])
+        for i, (frm, to) in enumerate(((pos_ref, pos_smem), (rows_ref, rows_smem)))
+    ]
+    to_smem[0].start()
     id_recv[0, 0:1, :] = id_send[0, 0:1, :]
     recvbuf[0:PER, :] = sendbuf[0:PER, :]
 
@@ -189,8 +207,7 @@
     for b in range(NB):
         got = jnp.concatenate([id_recv[8 * b + i, 0:1, :] for i in range(8)], axis=0)
         rows_ref[b : b + 1, :] = jnp.sum(jnp.where(keep, got, 0), axis=0, keepdims=True)
-    to_smem = pltpu.make_async_copy(rows_ref, rows_smem, smem_sem)
-    to_smem.start()
+    to_smem[1].start()
     for b in range(NB):
         row = rows_ref[b : b + 1, :].astype(F32)
         rcol[b * BLK : (b + 1) * BLK, :] = jnp.transpose(jnp.broadcast_to(row, (BLK, BLK)))
@@ -220,7 +237,8 @@
     lax.fori_loop(0, NB, build, 0)
 
     copies[3].wait()
-    to_smem.wait()
+    to_smem[0].wait()
+    to_smem[1].wait()
 
     def gather(b, c):
         base = pl.multiple_of(b * BLK, BLK)
@@ -231,34 +249,40 @@
 
     lax.fori_loop(0, NB, gather, 0)
 
-    many = pl.ds(0, (N - 1) * PER)
-    all_grads = remote(sendbuf.at[many], recvbuf.at[many], g_ssem, g_rsem, me)
-    all_grads.wait_send()
-    all_grads.wait_recv()
-
-    def split_recv(b, c):
-        at = pl.ds(pl.multiple_of(b * SB, SB), SB)
+    def split_recv(t):
+        at = pl.ds(pl.multiple_of(t * SB, SB), SB)
         hi, lo = split2(recvbuf[at, :])
         split[at, 0:W] = hi
         split[at, W : 2 * W] = lo
-        return c
-
-    lax.fori_loop(0, NSB, split_recv, 0)
-
-    def update(t):
+        return mm(eq[0:SB, at], split[at, :])
+
+    def arrived(lo, rows, sem):
+        at = pl.ds(lo, rows)
+        remote(sendbuf.at[at], recvbuf.at[at], g_ssem, sem, me).wait_recv()
+
+    arrived(PER, SB - PER, g_rsem.at[0])
+    first[...] = split_recv(0)
+
+    def take(t, c):
+        arrived(pl.multiple_of(t * SB, SB), SB, g_rsem.at[t])
+        first[...] += split_recv(t)
+        return c
+
+    lax.fori_loop(1, NSB, take, 0)
+
+    def update(t, both):
         at = pl.ds(pl.multiple_of(t * SB, SB), SB)
-        both = mm(eq[at, :], split[...])
         summed = both[:, 0:W] + both[:, W : 2 * W]
         msq = jnp.broadcast_to(jnp.sum(summed * summed, axis=1, keepdims=True), (SB, W)) * (1.0 / W)
         msq_col[at, :] = msq
         upd_ref[at, :] = emb[at, :] - LEARNING_RATE * summed / (jnp.sqrt(acc_col[at, :] + msq) + EPSILON)
 
     def update_send(t, c):
-        update(t)
+        update(t, mm(eq[pl.ds(pl.multiple_of(t * SB, SB), SB), :], split[...]))
         send_block(t, slot_rows(upd_ref), slot_rows(ret_ref), r_ssem, r_rsem, 0)
         return c
 
-    update(0)
+    update(0, first[...])
     send_block(0, slot_rows(upd_ref), slot_rows(ret_ref), r_ssem, r_rsem, 1)
     lax.fori_loop(1, NSB, update_send, 0)
     ret_ref[0:PER, :] = upd_ref[0:PER, :]
@@ -274,6 +298,8 @@
         delta = delta + mm(pick, t_hi) + mm(pick, t_mid) + mm(pick, t_lo)
     new_accum_ref[...] = accum_ref[...] + delta
 
+    many = pl.ds(0, (N - 1) * PER)
+    remote(sendbuf.at[many], recvbuf.at[many], g_ssem, g_rsem.at[0], me).wait_send()
     back = remote(upd_ref.at[many], ret_ref.at[many], r_ssem, r_rsem, me)
     back.wait_send()
     back.wait_recv()
@@ -319,15 +345,18 @@
 def on_device(lookup_ids, grad_rows, emb_table, row_accum):
     dma = pltpu.SemaphoreType.DMA
     f32 = lambda *s: jax.ShapeDtypeStruct(s, F32)
-    i32 = lambda *s: jax.ShapeDtypeStruct(s, I32)
+    smem = lambda *s: pltpu.SMEM(s, I32)
     vmem = lambda *s: pltpu.VMEM(s, F32)
     in_hbm = lambda a: pltpu.with_memory_space_constraint(a, pltpu.HBM)
     ret, upd, rows, pos, stepped, held = pl.pallas_call(
         exchange_kernel,
-        out_shape=(f32(LOOK, W), f32(LOOK, W), i32(NB, BLK), i32(NB, BLK), f32(N, BLK), vmem(ROWS, W)),
+        out_shape=(f32(LOOK, W), f32(LOOK, W), smem(NB, BLK), smem(NB, BLK), f32(N, BLK), vmem(ROWS, W)),
         in_specs=[HBM, HBM, HBM, HBM],
-        out_specs=(VM, VM, VM, VM, VM, VM),
+        out_specs=(VM, VM, SM, SM, VM, VM),
         scratch_shapes=[
+            pltpu.VMEM((NB, BLK), I32),
+            pltpu.VMEM((NB, BLK), I32),
+            pltpu.VMEM((SB, 2 * W), F32),
             pltpu.VMEM((NB, BLK), I32),
             pltpu.VMEM((LOOK, W), F32),
             pltpu.VMEM((N, BLK), F32),
@@ -342,9 +371,8 @@
             pltpu.VMEM((LOOK, W), F32),
             pltpu.VMEM((LOOK, W), F32),
             pltpu.VMEM((LOOK, W), F32),
-            pltpu.SMEM((NB, BLK), I32),
-            dma, dma, dma, dma, dma, dma, dma,
-            pltpu.SemaphoreType.DMA((4,)),
+            dma, dma, dma, pltpu.SemaphoreType.DMA((NSB,)), dma, dma,
+            pltpu.SemaphoreType.DMA((2,)), pltpu.SemaphoreType.DMA((4,)),
         ],
         compiler_params=pltpu.CompilerParams(
             collective_id=0, has_side_effects=True, vmem_limit_bytes=28 * 1024 * 1024

time: 51 us -> 50 us (0.980)
  Pallas kernels: 50.3 us -> 49.2 us
    pallas_call x1, Pallas kernels: 6.24 us -> 5.45 us  [on_device(): pl.pallas_call(place_kernel, out_shape=(f32(ROWS, W), f32(LOOK, W), f32(N...]
where the time goes in v3:
time: 50 us; the launch traced here: 49.9 us
  Pallas kernels  49.2 us (98%)
  between operations  0.64 us (1%)
    pallas_call x1, Pallas kernels, on_device(): pl.pallas_call(exchange_kernel, out_shape=(f32(LOOK, W), f32(LOOK, W), sm...  43.8 us
    pallas_call x1, Pallas kernels, on_device(): pl.pallas_call(place_kernel, out_shape=(f32(ROWS, W), f32(LOOK, W), f32(N...  5.45 us

profile of v3, /device:TPU:1, one launch (start us, length us, event | category | flops | bytes accessed | tf_op | source)
XLA Modules:
  0.0 49.9 jit_solution(3869416239406900761)
XLA Ops:
  0.6 43.8 %shard_map.67 = (f32[2048,128]{1,0:T(8,128)S(1)}, f32[2048,128]{1,0:T(8,128)S(1)}, s32[16,128]{1,0:T(8,128)S(4)}, s32[16,128]{1,0:T(8,128)S(4)}, f32[128,128]{1,0:T(8,128)S(1)}, /*index=5*/f32[16384,128]{1,0:T(8,128)S(1)}) custom-call(s32[16,128]{1,0:T(8,128)} %bitcast.4, f32[2048,128]{1,0:T(8,128)} %grads_hbm.1, f32[128,128]{1,0:T(8,128)} %bitcast.3, ...), custom_call_target="tpu_custom_call" | custom-call | tf_op jit(solution)/shard_map/pallas_call | solution.py:351
  44.4 5.5 %shard_map.68 = (f32[16384,128]{1,0:T(8,128)}, f32[2048,128]{1,0:T(8,128)}, f32[128,128]{1,0:T(8,128)}, f32[16384,128]{1,0:T(8,128)S(1)}) custom-call(f32[16384,128]{1,0:T(8,128)S(1)} %get-tuple-element.12.table_ref, f32[2048,128]{1,0:T(8,128)S(1)} %get-tuple-element.13.upd_ref, ...), custom_call_target="tpu_custom_call", output_to_operand_aliasing={{3}: (0, {})} | custom-call | tf_op jit(solution)/shard_map/pallas_call | solution.py:381

commit v4 on v3

--- a/solution.py
+++ b/solution.py
@@ -46,34 +46,14 @@
     return lax.dot_general(a, b, (((1,), (1,)), ((), ())), preferred_element_type=F32)
 
 
-SLOT_OFFSETS = (1, 42, 84, 48, 8, 2, 4)
-
-
-def offset_of(q):
-    out = 0
-    for i in range(4):
-        if (q >> i) & 1:
-            out ^= SLOT_OFFSETS[i]
-    return out
-
-
-def block_offset(t):
-    return (t & 1) * 8 + ((t >> 1) & 1) * 2 + ((t >> 2) & 1) * 4
-
-
 def hops(k):
     return sum((0, 1, 2, 1)[(k >> i) & 3] for i in (1, 3, 5))
 
 
-FAR_FIRST = sorted(range(1, N), key=lambda k: -hops(k))
-
-
-def slot_of(e):
-    bit = lambda i: (e >> i) & 1
-    q1 = bit(5) ^ bit(4) ^ bit(6)
-    q = bit(0) + (q1 << 1) + (bit(6) << 2) + ((bit(4) ^ bit(6)) << 3)
-    t = (bit(3) ^ q1) + ((bit(1) ^ q1) << 1) + ((bit(2) ^ bit(6)) << 2)
-    return q + (t << 4)
+OFFSETS = sorted(range(1, N), key=lambda k: (-hops(k), -(k & 1), k >> 5)) + [0]
+SELF = N - 1
+PICK = 512
+IDS_AT = 1
 
 
 def remote(src, dst, ssem, rsem, device):
@@ -85,14 +65,14 @@
 def exchange_kernel(
     ids_hbm, grads_hbm, accum_hbm, table_hbm,
     ret_ref, upd_ref, rows_smem, pos_smem, new_accum_ref, table,
-    rows_ref, pos_ref, first, ids_ref, grads_ref, accum_ref, sendbuf, recvbuf, id_send, id_recv, split, eq, emb, rcol, acc_col, cnt_col,
+    rows_ref, pos_ref, first, ids_ref, grads_ref, accum_ref, sendbuf, recvbuf, id_send, id_recv, split, eq, emb, rcol, acc_col, start_at,
     msq_col,
     id_ssem, id_rsem, g_ssem, g_rsem, r_ssem, r_rsem, smem_sem, in_sem,
 ):
     me = lax.axis_index("shard")
     barrier = pltpu.get_barrier_semaphore()
 
-    for k in FAR_FIRST:
+    for k in OFFSETS[:SELF]:
         pl.semaphore_signal(barrier, inc=1, device_id=(me ^ k,), device_id_type=MESH)
 
     copies = [
@@ -103,23 +83,20 @@
     ]
     for copy in copies[:3]:
         copy.start()
-    copies[0].wait()
 
     sub = iota((N, BLK), 0)
     lane = iota((N, BLK), 1)
     upper = onehot(sub <= lane)
-    carry = jnp.zeros((N, 1), F32)
-
-    def slots_at(b):
-        return slot_of(lax.shift_right_logical(ids_ref[b : b + 1, :], ROW_BITS) ^ me)
-
+    for k in range(N):
+        start_at[k : k + 1, :] = jnp.full((1, BLK), float(OFFSETS.index(k) * PER - 1), F32)
+    copies[0].wait()
+    carry = start_at[...]
     for b in range(NB):
-        slot = slots_at(b)
-        own = jnp.where(sub == slot, 1.0, 0.0)
-        count = mm(own.astype(BF16), upper) + carry
+        peer = lax.shift_right_logical(ids_ref[b : b + 1, :], ROW_BITS) ^ me
+        own = jnp.where(sub == peer, 1.0, 0.0)
+        place = mm(own.astype(BF16), upper) + carry
         carry = carry + jnp.sum(own, axis=1, keepdims=True)
-        rank = jnp.sum(own * count, axis=0, keepdims=True).astype(I32) - 1
-        pos_ref[b : b + 1, :] = slot * PER + rank
+        pos_ref[b : b + 1, :] = jnp.sum(own * place, axis=0, keepdims=True).astype(I32)
 
     def pack_ids():
         w_hi = jnp.zeros((N, BLK), F32)
@@ -158,45 +135,45 @@
             total = total + mm(pick, split[b * BLK : (b + 1) * BLK, :])
         sendbuf[pl.ds(base, SB), :] = total[:, 0:W] + total[:, W : 2 * W]
 
-    def send_block(t, frm, to, ssem, rsem, first):
-        far = me ^ block_offset(t)
-        for q in range(first, PEERS_SB):
+    def send_block(t, frm, to, ssem, rsem):
+        for q in range(PEERS_SB):
             slot = t * PEERS_SB + q
-            remote(frm(slot), to(slot), ssem, rsem, far ^ offset_of(q)).start()
+            if slot != SELF:
+                remote(frm(slot), to(slot), ssem, rsem, me ^ OFFSETS[slot]).start()
+
+    def send_block_at(t, *how):
+        for block in range(NSB):
+
+            @pl.when(t == block)
+            def _():
+                send_block(block, *how)
 
     def slot_rows(ref):
-        return lambda slot: ref.at[pl.ds(pl.multiple_of(slot * PER, PER), PER)]
-
-    def send_all(frm, to, ssem, rsem):
-        send_block(0, frm, to, ssem, rsem, 1)
-
-        def some(t, c):
-            send_block(t, frm, to, ssem, rsem, 0)
-            return c
-
-        lax.fori_loop(1, NSB, some, 0)
+        return lambda slot: ref.at[pl.ds(slot * PER, PER)]
 
     id_row = lambda ref: lambda slot: ref.at[slot, pl.ds(0, 1)]
 
     arrange(0)
     pl.semaphore_wait(barrier, N - 1)
-    send_block(0, slot_rows(sendbuf), slot_rows(recvbuf), g_ssem, g_rsem.at[0], 1)
-    pack_ids()
-    send_all(id_row(id_send), id_row(id_recv), id_ssem, id_rsem)
+    send_block(0, slot_rows(sendbuf), slot_rows(recvbuf), g_ssem, g_rsem.at[0])
 
     def arrange_send(t, c):
         arrange(t)
-        send_block(t, slot_rows(sendbuf), slot_rows(recvbuf), g_ssem, g_rsem.at[t], 0)
-        return c
-
-    lax.fori_loop(1, NSB, arrange_send, 0)
+        send_block_at(t, slot_rows(sendbuf), slot_rows(recvbuf), g_ssem, g_rsem.at[t])
+        return c
+
+    lax.fori_loop(1, IDS_AT, arrange_send, 0)
+    pack_ids()
+    for t in range(NSB):
+        send_block(t, id_row(id_send), id_row(id_recv), id_ssem, id_rsem)
+    lax.fori_loop(IDS_AT, NSB, arrange_send, 0)
+    id_recv[SELF, 0:1, :] = id_send[SELF, 0:1, :]
+    recvbuf[SELF * PER :, :] = sendbuf[SELF * PER :, :]
     to_smem = [
         pltpu.make_async_copy(frm, to, smem_sem.at[i])
         for i, (frm, to) in enumerate(((pos_ref, pos_smem), (rows_ref, rows_smem)))
     ]
     to_smem[0].start()
-    id_recv[0, 0:1, :] = id_send[0, 0:1, :]
-    recvbuf[0:PER, :] = sendbuf[0:PER, :]
 
     ids_all = remote(
         id_send.at[pl.ds(0, N - 1), pl.ds(0, 1)], id_recv.at[pl.ds(0, N - 1), pl.ds(0, 1)], id_ssem, id_rsem, me
@@ -213,41 +190,44 @@
         rcol[b * BLK : (b + 1) * BLK, :] = jnp.transpose(jnp.broadcast_to(row, (BLK, BLK)))
 
     copies[2].wait()
+    def build(b, c):
+        at = pl.ds(pl.multiple_of(b * BLK, BLK), BLK)
+        col = rcol[at, :]
+        for o in range(NB):
+            same = jnp.where(col == rows_ref[o : o + 1, :].astype(F32), 1.0, 0.0)
+            eq[at, o * BLK : (o + 1) * BLK] = same.astype(BF16)
+        return c
+
+    lax.fori_loop(0, NB, build, 0)
+
     acc_hi, acc_rest = split2(accum_ref[...])
     acc_lo = (accum_ref[...] - acc_hi.astype(F32) - acc_rest.astype(F32)).astype(BF16)
     acc3 = jnp.concatenate([acc_hi, acc_rest, acc_lo], axis=1)
 
-    def build(b, c):
-        at = pl.ds(pl.multiple_of(b * BLK, BLK), BLK)
-        col = rcol[at, :]
-        seen = jnp.zeros((BLK, BLK), F32)
-        for o in range(NB):
-            same = jnp.where(col == rows_ref[o : o + 1, :].astype(F32), 1.0, 0.0)
-            seen = seen + same
-            eq[at, o * BLK : (o + 1) * BLK] = same.astype(BF16)
-        cnt_col[at, :] = jnp.broadcast_to(jnp.sum(seen, axis=1, keepdims=True), (BLK, BLK))
-        num = col.astype(I32)
-        lanes = iota((BLK, BLK), 1)
+    def pick_accum(b, c):
+        at = pl.ds(pl.multiple_of(b * PICK, PICK), PICK)
+        num = rcol[at, :].astype(I32)
+        lanes = iota((PICK, BLK), 1)
         picked = mm(onehot((num >> 7) == lanes), acc3)
         picked = picked[:, 0:W] + picked[:, W : 2 * W] + picked[:, 2 * W :]
         acc = jnp.sum(jnp.where((num & 127) == lanes, picked, 0.0), axis=1, keepdims=True)
-        acc_col[at, :] = jnp.broadcast_to(acc, (BLK, BLK))
-        return c
-
-    lax.fori_loop(0, NB, build, 0)
+        acc_col[at, :] = jnp.broadcast_to(acc, (PICK, BLK))
+        return c
+
+    lax.fori_loop(0, LOOK // PICK, pick_accum, 0)
 
     copies[3].wait()
     to_smem[0].wait()
     to_smem[1].wait()
 
-    def gather(b, c):
-        base = pl.multiple_of(b * BLK, BLK)
-        for i in range(BLK):
-            r = rows_smem[b, i] & (ROWS - 1)
-            emb[pl.ds(base + i, 1), :] = table[pl.ds(r, 1), :]
-        return c
-
-    lax.fori_loop(0, NB, gather, 0)
+    def gather(t):
+        for h in range(SB // BLK):
+            base = pl.multiple_of(t * SB + h * BLK, BLK)
+            for i in range(BLK):
+                r = rows_smem[t * (SB // BLK) + h, i] & (ROWS - 1)
+                emb[pl.ds(base + i, 1), :] = table[pl.ds(r, 1), :]
+
+    gather(0)
 
     def split_recv(t):
         at = pl.ds(pl.multiple_of(t * SB, SB), SB)
@@ -260,7 +240,7 @@
         at = pl.ds(lo, rows)
         remote(sendbuf.at[at], recvbuf.at[at], g_ssem, sem, me).wait_recv()
 
-    arrived(PER, SB - PER, g_rsem.at[0])
+    arrived(0, SB, g_rsem.at[0])
     first[...] = split_recv(0)
 
     def take(t, c):
@@ -268,7 +248,9 @@
         first[...] += split_recv(t)
         return c
 
-    lax.fori_loop(1, NSB, take, 0)
+    lax.fori_loop(1, NSB - 1, take, 0)
+    arrived((NSB - 1) * SB, SB - PER, g_rsem.at[NSB - 1])
+    first[...] += split_recv(NSB - 1)
 
     def update(t, both):
         at = pl.ds(pl.multiple_of(t * SB, SB), SB)
@@ -278,20 +260,22 @@
         upd_ref[at, :] = emb[at, :] - LEARNING_RATE * summed / (jnp.sqrt(acc_col[at, :] + msq) + EPSILON)
 
     def update_send(t, c):
+        gather(t)
         update(t, mm(eq[pl.ds(pl.multiple_of(t * SB, SB), SB), :], split[...]))
-        send_block(t, slot_rows(upd_ref), slot_rows(ret_ref), r_ssem, r_rsem, 0)
+        send_block_at(t, slot_rows(upd_ref), slot_rows(ret_ref), r_ssem, r_rsem)
         return c
 
     update(0, first[...])
-    send_block(0, slot_rows(upd_ref), slot_rows(ret_ref), r_ssem, r_rsem, 1)
+    send_block(0, slot_rows(upd_ref), slot_rows(ret_ref), r_ssem, r_rsem)
     lax.fori_loop(1, NSB, update_send, 0)
-    ret_ref[0:PER, :] = upd_ref[0:PER, :]
+    ret_ref[SELF * PER :, :] = upd_ref[SELF * PER :, :]
 
     delta = jnp.zeros((N, BLK), F32)
     for b in range(NB):
         at = slice(b * BLK, (b + 1) * BLK)
         lo_row = rcol[at, :].astype(I32) & 127
-        term = jnp.where(lo_row == lane, msq_col[at, :] / cnt_col[at, :], 0.0)
+        count = mm(eq[at, :], jnp.ones((LOOK, BLK), BF16))
+        term = jnp.where(lo_row == lane, msq_col[at, :] / count, 0.0)
         t_hi, t_mid = split2(term)
         t_lo = (term - t_hi.astype(F32) - t_mid.astype(F32)).astype(BF16)
         pick = onehot((rows_ref[b : b + 1, :] >> 7) == sub)
@@ -369,7 +353,7 @@
             pltpu.VMEM((LOOK, W), F32),
             pltpu.VMEM((LOOK, W), F32),
             pltpu.VMEM((LOOK, W), F32),
-            pltpu.VMEM((LOOK, W), F32),
+            pltpu.VMEM((N, BLK), F32),
             pltpu.VMEM((LOOK, W), F32),
             dma, dma, dma, pltpu.SemaphoreType.DMA((NSB,)), dma, dma,
             pltpu.SemaphoreType.DMA((2,)), pltpu.SemaphoreType.DMA((4,)),

time: 50 us -> 48.9 us (0.978)
  Pallas kernels: 49.2 us -> 48.1 us
    pallas_call x1, Pallas kernels: 43.8 us -> 42.6 us  [on_device(): pl.pallas_call(exchange_kernel, out_shape=(f32(LOOK, W), f32(LOOK, W), sm...]
where the time goes in v4:
time: 48.9 us; the launch traced here: 48.7 us
  Pallas kernels  48.1 us (98%)
  between operations  0.64 us (1%)
    pallas_call x1, Pallas kernels, on_device(): pl.pallas_call(exchange_kernel, out_shape=(f32(LOOK, W), f32(LOOK, W), sm...  42.6 us
    pallas_call x1, Pallas kernels, on_device(): pl.pallas_call(place_kernel, out_shape=(f32(ROWS, W), f32(LOOK, W), f32(N...  5.45 us

profile of v4, /device:TPU:1, one launch (start us, length us, event | category | flops | bytes accessed | tf_op | source)
XLA Modules:
  0.0 48.7 jit_solution(9882377509999102067)
XLA Ops:
  0.6 42.6 %shard_map.67 = (f32[2048,128]{1,0:T(8,128)S(1)}, f32[2048,128]{1,0:T(8,128)S(1)}, s32[16,128]{1,0:T(8,128)S(4)}, s32[16,128]{1,0:T(8,128)S(4)}, f32[128,128]{1,0:T(8,128)S(1)}, /*index=5*/f32[16384,128]{1,0:T(8,128)S(1)}) custom-call(s32[16,128]{1,0:T(8,128)} %bitcast.4, f32[2048,128]{1,0:T(8,128)} %grads_hbm.1, f32[128,128]{1,0:T(8,128)} %bitcast.3, ...), custom_call_target="tpu_custom_call" | custom-call | tf_op jit(solution)/shard_map/pallas_call | solution.py:335
  43.3 5.5 %shard_map.68 = (f32[16384,128]{1,0:T(8,128)}, f32[2048,128]{1,0:T(8,128)}, f32[128,128]{1,0:T(8,128)}, f32[16384,128]{1,0:T(8,128)S(1)}) custom-call(f32[16384,128]{1,0:T(8,128)S(1)} %get-tuple-element.12.table_ref, f32[2048,128]{1,0:T(8,128)S(1)} %get-tuple-element.13.upd_ref, ...), custom_call_target="tpu_custom_call", output_to_operand_aliasing={{3}: (0, {})} | custom-call | tf_op jit(solution)/shard_map/pallas_call | solution.py:365

commit v5 on v4

--- a/solution.py
+++ b/solution.py
@@ -53,7 +53,8 @@
 OFFSETS = sorted(range(1, N), key=lambda k: (-hops(k), -(k & 1), k >> 5)) + [0]
 SELF = N - 1
 PICK = 512
-IDS_AT = 1
+PIECES = 8
+EARLY = 2
 
 
 def remote(src, dst, ssem, rsem, device):
@@ -153,20 +154,24 @@
 
     id_row = lambda ref: lambda slot: ref.at[slot, pl.ds(0, 1)]
 
-    arrange(0)
-    pl.semaphore_wait(barrier, N - 1)
-    send_block(0, slot_rows(sendbuf), slot_rows(recvbuf), g_ssem, g_rsem.at[0])
+    def arrange_only(t, c):
+        arrange(t)
+        return c
 
     def arrange_send(t, c):
         arrange(t)
         send_block_at(t, slot_rows(sendbuf), slot_rows(recvbuf), g_ssem, g_rsem.at[t])
         return c
 
-    lax.fori_loop(1, IDS_AT, arrange_send, 0)
     pack_ids()
+    lax.fori_loop(0, EARLY, arrange_only, 0)
+    pl.semaphore_wait(barrier, N - 1)
+    send_block(0, slot_rows(sendbuf), slot_rows(recvbuf), g_ssem, g_rsem.at[0])
     for t in range(NSB):
         send_block(t, id_row(id_send), id_row(id_recv), id_ssem, id_rsem)
-    lax.fori_loop(IDS_AT, NSB, arrange_send, 0)
+    for t in range(1, EARLY):
+        send_block(t, slot_rows(sendbuf), slot_rows(recvbuf), g_ssem, g_rsem.at[t])
+    lax.fori_loop(EARLY, NSB, arrange_send, 0)
     id_recv[SELF, 0:1, :] = id_send[SELF, 0:1, :]
     recvbuf[SELF * PER :, :] = sendbuf[SELF * PER :, :]
     to_smem = [
@@ -304,8 +309,11 @@
         return c
 
     lax.fori_loop(0, NB, scatter, 0)
-    table_out = pltpu.make_async_copy(table, new_table_ref, sems.at[1])
-    table_out.start()
+    table_out = []
+    for i in range(PIECES):
+        at = pl.ds(i * (ROWS // PIECES), ROWS // PIECES)
+        table_out.append(pltpu.make_async_copy(table.at[at], new_table_ref.at[at], sems.at[2 + i]))
+        table_out[-1].start()
 
     def unpermute(b, c):
         base = pl.multiple_of(b * BLK, BLK)
@@ -314,10 +322,11 @@
         return c
 
     lax.fori_loop(0, NB, unpermute, 0)
-    looked_out = pltpu.make_async_copy(looked, looked_ref, sems.at[2])
+    looked_out = pltpu.make_async_copy(looked, looked_ref, sems.at[1])
     looked_out.start()
     accum_out.wait()
-    table_out.wait()
+    for piece in table_out:
+        piece.wait()
     looked_out.wait()
 
 
@@ -368,7 +377,7 @@
         in_specs=[VM, VM, VM, SM, SM, VM],
         out_specs=(HBM, HBM, HBM, VM),
         input_output_aliases={0: 3},
-        scratch_shapes=[pltpu.VMEM((LOOK, W), F32), pltpu.SemaphoreType.DMA((3,))],
+        scratch_shapes=[pltpu.VMEM((LOOK, W), F32), pltpu.SemaphoreType.DMA((2 + PIECES,))],
         compiler_params=pltpu.CompilerParams(vmem_limit_bytes=4 * 1024 * 1024),
     )(held, upd, ret, rows, pos, stepped)
     return (new_table, new_accum.reshape(ROWS), looked_up)

time: 48.9 us -> 48.6 us (level)
  no operation moved by 1% of the time
where the time goes in v5:
time: 48.6 us; the launch traced here: 48.5 us
  Pallas kernels  47.8 us (98%)
  between operations  0.64 us (1%)
    pallas_call x1, Pallas kernels, on_device(): pl.pallas_call(exchange_kernel, out_shape=(f32(LOOK, W), f32(LOOK, W), sm...  42.4 us
    pallas_call x1, Pallas kernels, on_device(): pl.pallas_call(place_kernel, out_shape=(f32(ROWS, W), f32(LOOK, W), f32(N...  5.39 us

profile of v5, /device:TPU:1, one launch (start us, length us, event | category | flops | bytes accessed | tf_op | source)
XLA Modules:
  0.0 48.5 jit_solution(7012736341998990517)
XLA Ops:
  0.6 42.4 %shard_map.67 = (f32[2048,128]{1,0:T(8,128)S(1)}, f32[2048,128]{1,0:T(8,128)S(1)}, s32[16,128]{1,0:T(8,128)S(4)}, s32[16,128]{1,0:T(8,128)S(4)}, f32[128,128]{1,0:T(8,128)S(1)}, /*index=5*/f32[16384,128]{1,0:T(8,128)S(1)}) custom-call(s32[16,128]{1,0:T(8,128)} %bitcast.4, f32[2048,128]{1,0:T(8,128)} %grads_hbm.1, f32[128,128]{1,0:T(8,128)} %bitcast.3, ...), custom_call_target="tpu_custom_call" | custom-call | tf_op jit(solution)/shard_map/pallas_call | solution.py:344
  43.1 5.4 %shard_map.68 = (f32[16384,128]{1,0:T(8,128)}, f32[2048,128]{1,0:T(8,128)}, f32[128,128]{1,0:T(8,128)}, f32[16384,128]{1,0:T(8,128)S(1)}) custom-call(f32[16384,128]{1,0:T(8,128)S(1)} %get-tuple-element.12.table_ref, f32[2048,128]{1,0:T(8,128)S(1)} %get-tuple-element.13.upd_ref, ...), custom_call_target="tpu_custom_call", output_to_operand_aliasing={{3}: (0, {})} | custom-call | tf_op jit(solution)/shard_map/pallas_call | solution.py:374

commit v6 on v5

--- a/solution.py
+++ b/solution.py
@@ -54,6 +54,7 @@
 SELF = N - 1
 PICK = 512
 PIECES = 8
+AHEAD = 4
 EARLY = 2
 
 
@@ -253,7 +254,12 @@
         first[...] += split_recv(t)
         return c
 
-    lax.fori_loop(1, NSB - 1, take, 0)
+    def gather_take(t, c):
+        gather(t)
+        return take(t, c)
+
+    lax.fori_loop(1, AHEAD, gather_take, 0)
+    lax.fori_loop(AHEAD, NSB - 1, take, 0)
     arrived((NSB - 1) * SB, SB - PER, g_rsem.at[NSB - 1])
     first[...] += split_recv(NSB - 1)
 
@@ -265,14 +271,18 @@
         upd_ref[at, :] = emb[at, :] - LEARNING_RATE * summed / (jnp.sqrt(acc_col[at, :] + msq) + EPSILON)
 
     def update_send(t, c):
-        gather(t)
         update(t, mm(eq[pl.ds(pl.multiple_of(t * SB, SB), SB), :], split[...]))
         send_block_at(t, slot_rows(upd_ref), slot_rows(ret_ref), r_ssem, r_rsem)
         return c
 
     update(0, first[...])
     send_block(0, slot_rows(upd_ref), slot_rows(ret_ref), r_ssem, r_rsem)
-    lax.fori_loop(1, NSB, update_send, 0)
+    def gather_update_send(t, c):
+        gather(t)
+        return update_send(t, c)
+
+    lax.fori_loop(1, AHEAD, update_send, 0)
+    lax.fori_loop(AHEAD, NSB, gather_update_send, 0)
     ret_ref[SELF * PER :, :] = upd_ref[SELF * PER :, :]
 
     delta = jnp.zeros((N, BLK), F32)

time: 48.6 us -> 48.6 us (level)
  no operation moved by 1% of the time
where the time goes in v6:
time: 48.6 us; the launch traced here: 48.5 us
  Pallas kernels  47.8 us (98%)
  between operations  0.64 us (1%)
    pallas_call x1, Pallas kernels, on_device(): pl.pallas_call(exchange_kernel, out_shape=(f32(LOOK, W), f32(LOOK, W), sm...  42.5 us
    pallas_call x1, Pallas kernels, on_device(): pl.pallas_call(place_kernel, out_shape=(f32(ROWS, W), f32(LOOK, W), f32(N...  5.39 us

profile of v6, /device:TPU:1, one launch (start us, length us, event | category | flops | bytes accessed | tf_op | source)
XLA Modules:
  0.0 48.5 jit_solution(12828094852938990361)
XLA Ops:
  0.6 42.5 %shard_map.67 = (f32[2048,128]{1,0:T(8,128)S(1)}, f32[2048,128]{1,0:T(8,128)S(1)}, s32[16,128]{1,0:T(8,128)S(4)}, s32[16,128]{1,0:T(8,128)S(4)}, f32[128,128]{1,0:T(8,128)S(1)}, /*index=5*/f32[16384,128]{1,0:T(8,128)S(1)}) custom-call(s32[16,128]{1,0:T(8,128)} %bitcast.4, f32[2048,128]{1,0:T(8,128)} %grads_hbm.1, f32[128,128]{1,0:T(8,128)} %bitcast.3, ...), custom_call_target="tpu_custom_call" | custom-call | tf_op jit(solution)/shard_map/pallas_call | solution.py:354
  43.1 5.4 %shard_map.68 = (f32[16384,128]{1,0:T(8,128)}, f32[2048,128]{1,0:T(8,128)}, f32[128,128]{1,0:T(8,128)}, f32[16384,128]{1,0:T(8,128)S(1)}) custom-call(f32[16384,128]{1,0:T(8,128)S(1)} %get-tuple-element.12.table_ref, f32[2048,128]{1,0:T(8,128)S(1)} %get-tuple-element.13.upd_ref, ...), custom_call_target="tpu_custom_call", output_to_operand_aliasing={{3}: (0, {})} | custom-call | tf_op jit(solution)/shard_map/pallas_call | solution.py:384
